TPU v7x, 32 devices: a whole 2x2x4 slice. The times are simulated.
32 devices in a mesh: shard: 8 (over y, x, core), tensor: 4 (over z).
Axes of the slice: x: 2, y: 2, z: 4, core: 2. Of those that a mesh axis runs over, the one named last changes fastest.
Arguments:
- tokens: bfloat16 [16384, 2048], P('shard'), may hold values from -40 to 40
- ln1_gain: bfloat16 [2048], P('shard'), may hold values from 0.25 to 1.75
- ln1_bias: bfloat16 [2048], P('shard'), may hold values from -3 to 3
- qkv_weight: bfloat16 [2048, 8, 3, 256], P('shard', 'tensor'), may hold values from -2 to 2
- qkv_bias: bfloat16 [8, 3, 256], P('tensor'), may hold values from -3 to 3
- out_weight: bfloat16 [2048, 8, 256], P('shard', 'tensor'), may hold values from -0.5 to 0.5
- out_bias: bfloat16 [2048], P('shard'), may hold values from -3 to 3
- ln2_gain: bfloat16 [2048], P('shard'), may hold values from 0.25 to 1.75
- ln2_bias: bfloat16 [2048], P('shard'), may hold values from -3 to 3
- fc1_weight: bfloat16 [2048, 8192], P('shard', 'tensor'), may hold values from -0.125 to 0.125
- fc1_bias: bfloat16 [8192], P('tensor'), may hold values from -3 to 3
- fc2_weight: bfloat16 [2048, 8192], P('shard', 'tensor'), may hold values from -0.0625 to 0.0625
- fc2_bias: bfloat16 [2048], P('shard'), may hold values from -3 to 3
- cotangent: bfloat16 [16384, 2048], P('shard'), may hold values from -6 to 6
Outputs:
- block_out: bfloat16 [16384, 2048], P('shard')
- grad_tokens: float32 [16384, 2048], P('shard')
- grad_ln1_gain: float32 [2048], P('shard')
- grad_ln1_bias: float32 [2048], P('shard')
- grad_qkv_weight: float32 [2048, 8, 3, 256], P('shard', 'tensor')
- grad_qkv_bias: float32 [8, 3, 256], P('tensor')
- grad_out_weight: float32 [2048, 8, 256], P('shard', 'tensor')
- grad_out_bias: float32 [2048], P('shard')
- grad_ln2_gain: float32 [2048], P('shard')
- grad_ln2_bias: float32 [2048], P('shard')
- grad_fc1_weight: float32 [2048, 8192], P('shard', 'tensor')
- grad_fc1_bias: float32 [8192], P('tensor')
- grad_fc2_weight: float32 [2048, 8192], P('shard', 'tensor')
- grad_fc2_bias: float32 [2048], P('shard')
All inputs are finite; a program needn't handle non-finite values.
Results may differ from a plain program's by a relative error of at most 0.017.
Values may be sent and summed in bfloat16 or wider, within the bound.
A program may use at most 320 MiB of HBM per device.

v0:
```python
import math
import jax
import jax.numpy as jnp
from jax import lax
from jax.sharding import PartitionSpec as P

ROT = 64
SEQ = 256
MICRO = 2
NORM_EPS = 1e-05
ROOT_HALF = 0.7071067811865476
INV_ROOT_TWO_PI = 0.3989422804014327


def as_sent(shard):

    def short(part):
        return part.astype(jnp.bfloat16) if part.dtype == jnp.float32 else part

    return jax.tree.map(short, shard)


def normalize(residual):
    row_mean = jnp.mean(residual, axis=-1, keepdims=True)
    centered = residual - row_mean
    row_var = jnp.mean(centered * centered, axis=-1, keepdims=True)
    inv_std = lax.rsqrt(row_var + NORM_EPS)
    return (centered * inv_std, inv_std)


def norm_backward(grad_normed, gain_wide, normalized, inv_std):
    scaled_grad = grad_normed * gain_wide
    return inv_std * (
        scaled_grad
        - jnp.mean(scaled_grad, axis=-1, keepdims=True)
        - normalized * jnp.mean(scaled_grad * normalized, axis=-1, keepdims=True)
    )


def rotary_tables(length, rot_dims):
    half_dims = rot_dims // 2
    frequency = jnp.power(10000.0, -2.0 * jnp.arange(half_dims, dtype=jnp.float32) / rot_dims)
    angles = jnp.arange(length, dtype=jnp.float32)[:, None] * frequency[None, :]
    return (jnp.cos(angles), jnp.sin(angles))


def rotate(field, cos_tab, sin_tab, rot_dims):
    half_dims = rot_dims // 2
    lower_half = field[..., :half_dims]
    upper_half = field[..., half_dims:rot_dims]
    cos_wide = cos_tab[None, :, None, :]
    sin_wide = sin_tab[None, :, None, :]
    return jnp.concatenate(
        [
            lower_half * cos_wide - upper_half * sin_wide,
            upper_half * cos_wide + lower_half * sin_wide,
            field[..., rot_dims:],
        ],
        axis=-1,
    )


def rotate_back(grad_field, cos_tab, sin_tab, rot_dims):
    half_dims = rot_dims // 2
    lower_half = grad_field[..., :half_dims]
    upper_half = grad_field[..., half_dims:rot_dims]
    cos_wide = cos_tab[None, :, None, :]
    sin_wide = sin_tab[None, :, None, :]
    return jnp.concatenate(
        [
            lower_half * cos_wide + upper_half * sin_wide,
            upper_half * cos_wide - lower_half * sin_wide,
            grad_field[..., rot_dims:],
        ],
        axis=-1,
    )


def gelu_exact(pre_act):
    return 0.5 * pre_act * (1.0 + lax.erf(pre_act * ROOT_HALF))


def gelu_slope(pre_act):
    return (
        0.5 * (1.0 + lax.erf(pre_act * ROOT_HALF))
        + pre_act * jnp.exp(-0.5 * pre_act * pre_act) * INV_ROOT_TWO_PI
    )


def causal_scores(queries, key_rows, score_scale):
    length = queries.shape[1]
    scores = (
        jnp.einsum("nqhc,nkhc->nhqk", queries, key_rows, preferred_element_type=jnp.float32)
        * score_scale
    )
    causal = jnp.arange(length)[:, None] >= jnp.arange(length)[None, :]
    return jnp.where(causal[None, None], scores, -1e30)


def add_pairs(older, newer):
    return tuple((first_term + second_term for first_term, second_term in zip(older, newer)))


def forward_pass(x_block, weights, qkv_shift, fc1_shift, cos_tab, sin_tab):
    (
        qkv_full,
        out_full,
        fc1_full,
        fc2_full,
        gain_one,
        bias_one,
        gain_two,
        bias_two,
        out_shift,
        fc2_shift,
    ) = weights
    row_count = x_block.shape[0]
    seq_count = row_count // SEQ
    head_count = qkv_full.shape[1]
    head_dim = qkv_full.shape[3]
    residual = x_block.astype(jnp.float32)
    normalized, inv_std = normalize(residual)
    normed_one = (normalized * gain_one.astype(jnp.float32) + bias_one.astype(jnp.float32)).astype(
        jnp.bfloat16
    )
    normed_two = (normalized * gain_two.astype(jnp.float32) + bias_two.astype(jnp.float32)).astype(
        jnp.bfloat16
    )
    qkv = jnp.einsum("md,dhkc->mhkc", normed_one, qkv_full, preferred_element_type=jnp.float32)
    qkv = qkv + qkv_shift.astype(jnp.float32)
    fields = qkv.reshape(seq_count, SEQ, head_count, 3, head_dim)
    queries = rotate(fields[:, :, :, 0], cos_tab, sin_tab, ROT).astype(jnp.bfloat16)
    key_rows = rotate(fields[:, :, :, 1], cos_tab, sin_tab, ROT).astype(jnp.bfloat16)
    values = fields[:, :, :, 2].astype(jnp.bfloat16)
    score_scale = 1.0 / math.sqrt(head_dim)
    scores = causal_scores(queries, key_rows, score_scale)
    row_top = jnp.max(scores, axis=-1, keepdims=True)
    log_total = row_top + jnp.log(jnp.sum(jnp.exp(scores - row_top), axis=-1, keepdims=True))
    attn_probs = jnp.exp(scores - log_total).astype(jnp.bfloat16)
    attn_out = jnp.einsum("nhqk,nkhc->nqhc", attn_probs, values, preferred_element_type=jnp.float32)
    attn_out = attn_out.astype(jnp.bfloat16).reshape(row_count, head_count, head_dim)
    pre_act = jnp.dot(normed_two, fc1_full, preferred_element_type=jnp.float32) + fc1_shift.astype(
        jnp.float32
    )
    hidden = gelu_exact(pre_act).astype(jnp.bfloat16)
    partial_value = jnp.einsum(
        "mhc,dhc->md", attn_out, out_full, preferred_element_type=jnp.float32
    )
    partial_value = partial_value + jnp.einsum(
        "mf,df->md", hidden, fc2_full, preferred_element_type=jnp.float32
    )
    saved = (
        residual,
        normalized,
        inv_std,
        normed_one,
        normed_two,
        queries,
        key_rows,
        values,
        log_total,
        attn_out,
        pre_act,
        hidden,
    )
    return (partial_value, saved)


def backward_pass(grad_block, saved, weights, cos_tab, sin_tab):
    (
        qkv_full,
        out_full,
        fc1_full,
        fc2_full,
        gain_one,
        bias_one,
        gain_two,
        bias_two,
        out_shift,
        fc2_shift,
    ) = weights
    (
        residual,
        normalized,
        inv_std,
        normed_one,
        normed_two,
        queries,
        key_rows,
        values,
        log_total,
        attn_out,
        pre_act,
        hidden,
    ) = saved
    row_count = grad_block.shape[0]
    seq_count = row_count // SEQ
    head_count = qkv_full.shape[1]
    head_dim = qkv_full.shape[3]
    score_scale = 1.0 / math.sqrt(head_dim)
    grad_wide = grad_block.astype(jnp.float32)
    shift_grad = jnp.sum(grad_wide, axis=0)
    grad_out_w = jnp.einsum("md,mhc->dhc", grad_block, attn_out, preferred_element_type=jnp.float32)
    grad_fc2_w = jnp.einsum("md,mf->df", grad_block, hidden, preferred_element_type=jnp.float32)
    d_attn = jnp.einsum("md,dhc->mhc", grad_block, out_full, preferred_element_type=jnp.float32)
    d_attn = d_attn.astype(jnp.bfloat16).reshape(seq_count, SEQ, head_count, head_dim)
    d_pre = jnp.dot(grad_block, fc2_full, preferred_element_type=jnp.float32) * gelu_slope(pre_act)
    fc1_shift_grad = jnp.sum(d_pre, axis=0)
    d_pre_b = d_pre.astype(jnp.bfloat16)
    grad_fc1_w = jnp.einsum("md,mf->df", normed_two, d_pre_b, preferred_element_type=jnp.float32)
    d_two = jnp.einsum("mf,df->md", d_pre_b, fc1_full, preferred_element_type=jnp.float32)
    probs_again = jnp.exp(causal_scores(queries, key_rows, score_scale) - log_total)
    d_values = jnp.einsum(
        "nhqk,nqhc->nkhc",
        probs_again.astype(jnp.bfloat16),
        d_attn,
        preferred_element_type=jnp.float32,
    )
    d_probs = jnp.einsum("nqhc,nkhc->nhqk", d_attn, values, preferred_element_type=jnp.float32)
    row_delta = jnp.sum(probs_again * d_probs, axis=-1, keepdims=True)
    d_scores = (probs_again * (d_probs - row_delta) * score_scale).astype(jnp.bfloat16)
    d_queries = rotate_back(
        jnp.einsum("nhqk,nkhc->nqhc", d_scores, key_rows, preferred_element_type=jnp.float32),
        cos_tab,
        sin_tab,
        ROT,
    )
    d_keys = rotate_back(
        jnp.einsum("nhqk,nqhc->nkhc", d_scores, queries, preferred_element_type=jnp.float32),
        cos_tab,
        sin_tab,
        ROT,
    )
    d_qkv = jnp.stack([d_queries, d_keys, d_values], axis=3).reshape(
        row_count, head_count, 3, head_dim
    )
    qkv_shift_grad = jnp.sum(d_qkv, axis=0)
    d_qkv_b = d_qkv.astype(jnp.bfloat16)
    grad_qkv_w = jnp.einsum(
        "md,mhkc->dhkc", normed_one, d_qkv_b, preferred_element_type=jnp.float32
    )
    d_one = jnp.einsum("mhkc,dhkc->md", d_qkv_b, qkv_full, preferred_element_type=jnp.float32)
    d_input = norm_backward(
        d_one, gain_one.astype(jnp.float32), normalized, inv_std
    ) + norm_backward(d_two, gain_two.astype(jnp.float32), normalized, inv_std)
    norm_terms = jnp.stack(
        [
            jnp.sum(d_one * normalized, axis=0),
            jnp.sum(d_one, axis=0),
            jnp.sum(d_two * normalized, axis=0),
            jnp.sum(d_two, axis=0),
        ]
    )
    matrix_grads = (grad_qkv_w, grad_out_w, grad_fc1_w, grad_fc2_w)
    return (d_input, norm_terms, matrix_grads, shift_grad, qkv_shift_grad, fc1_shift_grad)


def per_device(
    tokens,
    ln1_gain,
    ln1_bias,
    qkv_weight,
    qkv_bias,
    out_weight,
    out_bias,
    ln2_gain,
    ln2_bias,
    fc1_weight,
    fc1_bias,
    fc2_weight,
    fc2_bias,
    cotangent,
):
    own_shards = (
        qkv_weight,
        out_weight,
        fc1_weight,
        fc2_weight,
        ln1_gain,
        ln1_bias,
        ln2_gain,
        ln2_bias,
        out_bias,
        fc2_bias,
    )
    micro_rows = tokens.shape[0] // MICRO
    cos_tab, sin_tab = rotary_tables(SEQ, ROT)
    outputs = []
    grad_outputs = []
    grad_accum = None
    qkv_shift_acc = jnp.zeros(qkv_bias.shape, jnp.float32)
    fc1_shift_acc = jnp.zeros(fc1_bias.shape, jnp.float32)
    for micro_index in range(MICRO):
        x_block = tokens[micro_index * micro_rows : (micro_index + 1) * micro_rows]
        grad_block = cotangent[micro_index * micro_rows : (micro_index + 1) * micro_rows]
        forward_weights = (
            lax.all_gather(own_shards[0], "shard", axis=0, tiled=True),
            lax.all_gather(own_shards[1], "shard", axis=0, tiled=True),
            lax.all_gather(own_shards[2], "shard", axis=0, tiled=True),
            lax.all_gather(own_shards[3], "shard", axis=0, tiled=True),
            lax.all_gather(own_shards[4], "shard", axis=0, tiled=True),
            lax.all_gather(own_shards[5], "shard", axis=0, tiled=True),
            lax.all_gather(own_shards[6], "shard", axis=0, tiled=True),
            lax.all_gather(own_shards[7], "shard", axis=0, tiled=True),
            lax.all_gather(own_shards[8], "shard", axis=0, tiled=True),
            lax.all_gather(own_shards[9], "shard", axis=0, tiled=True),
        )
        partial_value, saved = forward_pass(
            x_block, forward_weights, qkv_bias, fc1_bias, cos_tab, sin_tab
        )
        branch_total = lax.psum(partial_value.astype(jnp.bfloat16), "tensor").astype(jnp.float32)
        shifts = forward_weights[8].astype(jnp.float32) + forward_weights[9].astype(jnp.float32)
        outputs.append((saved[0] + branch_total + shifts).astype(jnp.bfloat16))
        backward_weights = (
            lax.all_gather(own_shards[0], "shard", axis=0, tiled=True),
            lax.all_gather(own_shards[1], "shard", axis=0, tiled=True),
            lax.all_gather(own_shards[2], "shard", axis=0, tiled=True),
            lax.all_gather(own_shards[3], "shard", axis=0, tiled=True),
            lax.all_gather(own_shards[4], "shard", axis=0, tiled=True),
            lax.all_gather(own_shards[5], "shard", axis=0, tiled=True),
            lax.all_gather(own_shards[6], "shard", axis=0, tiled=True),
            lax.all_gather(own_shards[7], "shard", axis=0, tiled=True),
            lax.all_gather(own_shards[8], "shard", axis=0, tiled=True),
            lax.all_gather(own_shards[9], "shard", axis=0, tiled=True),
        )
        d_input, norm_terms, matrix_grads, shift_grad, qkv_shift_grad, fc1_shift_grad = (
            backward_pass(grad_block, saved, backward_weights, cos_tab, sin_tab)
        )
        summed_input, summed_norms = (
            lax.psum(d_input.astype(jnp.bfloat16), "tensor").astype(jnp.float32),
            lax.psum(norm_terms.astype(jnp.bfloat16), "tensor").astype(jnp.float32),
        )
        grad_outputs.append(grad_block.astype(jnp.float32) + summed_input)
        grad_terms = matrix_grads + (
            summed_norms[0],
            summed_norms[1],
            summed_norms[2],
            summed_norms[3],
            shift_grad,
        )
        grad_accum = grad_terms if micro_index == 0 else add_pairs(grad_accum, grad_terms)
        qkv_shift_acc = qkv_shift_acc + qkv_shift_grad
        fc1_shift_acc = fc1_shift_acc + fc1_shift_grad
    shares = jax.tree.map(
        lambda part: part.astype(jnp.float32),
        lax.psum_scatter(as_sent(grad_accum), "shard", scatter_dimension=0, tiled=True),
    )
    qkv_shift_sum, fc1_shift_sum = lax.psum((qkv_shift_acc, fc1_shift_acc), "shard")
    return (
        jnp.concatenate(outputs, axis=0),
        jnp.concatenate(grad_outputs, axis=0),
        shares[4],
        shares[5],
        shares[0],
        qkv_shift_sum,
        shares[1],
        shares[8],
        shares[6],
        shares[7],
        shares[2],
        fc1_shift_sum,
        shares[3],
        shares[8],
    )


def solution(mesh):
    return jax.shard_map(
        per_device,
        mesh=mesh,
        in_specs=(
            P("shard", None),
            P("shard"),
            P("shard"),
            P("shard", "tensor", None, None),
            P("tensor", None, None),
            P("shard", "tensor", None),
            P("shard"),
            P("shard"),
            P("shard"),
            P("shard", "tensor"),
            P("tensor"),
            P("shard", "tensor"),
            P("shard"),
            P("shard", None),
        ),
        out_specs=(
            P("shard", None),
            P("shard", None),
            P("shard"),
            P("shard"),
            P("shard", "tensor", None, None),
            P("tensor", None, None),
            P("shard", "tensor", None),
            P("shard"),
            P("shard"),
            P("shard"),
            P("shard", "tensor"),
            P("tensor"),
            P("shard", "tensor"),
            P("shard"),
        ),
        check_vma=False,
    )
```

profile of v0, /device:TPU:0, one launch (start us, length us, event | category | flops | bytes accessed | tf_op | source)
XLA Modules:
  0.0 1115.3 jit_solution(9230165923432377804)
XLA Ops:
  12.7 10.4 all-gather.3
  23.7 8.9 all-gather.2
  41.3 8.9 all-gather
  71.8 17.2 %all-gather.11.cloned.1.call-done = bf16[2048,2,3,256]{3,0,2,1:T(8,128)(2,1)} async-done(((bf16[256,2,3,256]{3,0,2,1:T(8,128)(2,1)}), bf16[2048,2,3,256]{3,0,2,1:T(8,128)(2,1)}) %all-gather.11.cloned.1.call-update) | async-done | bytes 6291472 | tf_op jit(solution)/shard_map/all_gather | solution.py:297
  89.0 11.2 %broadcast_add_fusion = f32[1024,2,3,256]{3,0,2,1:T(8,128)S(1)} fusion(f32[2,3,256]{2,1,0:T(4,128)S(1)} %copy.111, bf16[2048,2,3,256]{3,0,2,1:T(8,128)(2,1)} %all-gather.11.cloned.1.call-done, f32[1024]{0:T(1024)S(1)} %add_rsqrt_fusion, f32[1024]{0:T(1024)S(1)} %get-tuple-element.149, f32[2048]{0:T(1024)S(1)} %bitcast.255, f32[2048]{0:T(1024)S(1)} %bitcast.239, ...), kind=kOutput, calls=%fused_computation.115 | convolution fusion | flops 6456606720 | bytes 16807936 | tf_op jit(solution)/shard_map/md,dhkc->mhkc/dot_general | solution.py:129
  177.8 14.8 %fusion.146 = f32[2048,2,3,256]{3,0,2,1:T(8,128)} fusion(f32[2048]{0:T(1024)S(1)} %bitcast.257, f32[2048]{0:T(1024)S(1)} %bitcast.241, f32[1024]{0:T(1024)S(1)} %add_rsqrt_fusion.1, f32[1024]{0:T(1024)S(1)} %get-tuple-element.150, f32[1024,2,1,256]{3,0,2,1:T(8,128)} %bitcast.198, f32[1024,2,1,256]{3,0,2,1:T(8,128)} %bitcast.201, ...), kind=kOutput, calls=%fused_computation.178 | convolution fusion | flops 6464471040 | bytes 23093248 | tf_op jit(solution)/shard_map/md,mhkc->dhkc/dot_general | solution.py:239
  205.5 15.2 %add_convert_fusion.2 = bf16[2048,2,3,256]{3,0,2,1:T(8,128)(2,1)} fusion(f32[2048,2,3,256]{3,0,2,1:T(8,128)} %fusion.146, f32[1024]{0:T(1024)S(1)} %add_rsqrt_fusion, f32[1024]{0:T(1024)S(1)} %get-tuple-element.149, f32[2048]{0:T(1024)S(1)} %bitcast.258, f32[2048]{0:T(1024)S(1)} %bitcast.242, f32[1024,2,1,256]{3,0,2,1:T(8,128)S(1)} %bitcast.207, ...), kind=kOutput, calls=%fused_computation.5 | convolution fusion | flops 6470762496 | bytes 29384704 | tf_op jit(solution)/shard_map/md,mhkc->dhkc/dot_general | solution.py:239
  221.5 12.8 %fusion.209 = f32[1024,2048]{1,0:T(8,128)S(1)} fusion(bf16[2048,2048]{1,0:T(8,128)(2,1)} %all-gather.15.cloned.1.call-done, f32[1024]{0:T(1024)S(1)} %add_rsqrt_fusion, f32[1024]{0:T(1024)S(1)} %get-tuple-element.149, f32[2048]{0:T(1024)S(1)} %bitcast.251, f32[2048]{0:T(1024)S(1)} %bitcast.232, bf16[2048,2048]{1,0:T(8,128)(2,1)} %param.14), kind=kOutput, calls=%fused_computation.270 | convolution fusion | flops 8602517504 | bytes 20996096 | tf_op jit(solution)/shard_map/dot_general | solution.py:142
  237.5 15.7 %multiply_convert_fusion.1 = (bf16[1024,2048]{1,0:T(8,128)(2,1)}, bf16[1024,2048]{1,0:T(8,128)(2,1)}, f32[1024,2048]{1,0:T(8,128)}) fusion(f32[2048]{0:T(1024)S(1)} %copy-done.43, f32[1024,2048]{1,0:T(8,128)S(1)} %fusion.209, bf16[2048,2048]{1,0:T(8,128)(2,1)S(1)} %copy-done.49, f32[2048]{0:T(1024)S(1)} %bitcast.252, f32[2048]{0:T(1024)S(1)} %bitcast.233, ...), kind=kOutput, calls=%fused_computation.92 | convolution fusion | flops 8627683328 | bytes 37781504 | tf_op jit(solution)/shard_map/dot_general | solution.py:142
  253.1 18.4 %fusion.215 = (f32[2048]{0:T(1024)}, bf16[1024,2048]{1,0:T(8,128)(2,1)S(1)}) fusion(f32[1024,2048]{1,0:T(8,128)} %get-tuple-element.139, f32[2048]{0:T(1024)S(1)} %copy-done.43, bf16[2048,2048]{1,0:T(8,128)(2,1)} %all-gather.17.cloned.1.call-done, bf16[2048,2048]{1,0:T(8,128)(2,1)} %param.27), kind=kOutput, calls=%fused_computation.275 | convolution fusion | flops 8615098368 | bytes 25182208 | tf_op jit(solution)/shard_map/dot_general | solution.py:207
  271.5 16.8 %fusion.92 = f32[2048,2048]{1,0:T(8,128)} fusion(bf16[1024,2048]{1,0:T(8,128)(2,1)S(1)} %get-tuple-element.146, f32[2048]{0:T(1024)S(1)} %bitcast.253, f32[2048]{0:T(1024)S(1)} %bitcast.234, f32[1024]{0:T(1024)S(1)} %add_rsqrt_fusion.1, f32[1024]{0:T(1024)S(1)} %get-tuple-element.150, bf16[2048,2048]{1,0:T(8,128)(2,1)} %param.14), kind=kOutput, calls=%fused_computation.138 | convolution fusion | flops 8602517504 | bytes 25190400 | tf_op jit(solution)/shard_map/md,mf->df/dot_general | solution.py:210
  288.3 16.6 %fusion.216 = (f32[2048]{0:T(1024)}, bf16[1024,2048]{1,0:T(8,128)(2,1)}) fusion(f32[1024,2048]{1,0:T(8,128)} %copy-done.59, f32[2048]{0:T(1024)S(1)} %copy-done.43, bf16[2048,2048]{1,0:T(8,128)(2,1)S(1)} %copy-done.48, bf16[2048,2048]{1,0:T(8,128)(2,1)} %param.27), kind=kOutput, calls=%fused_computation.276 | convolution fusion | flops 8615098368 | bytes 25182208 | tf_op jit(solution)/shard_map/dot_general | solution.py:207
  305.0 16.8 %add_convert_fusion.1 = bf16[2048,2048]{1,0:T(8,128)(2,1)} fusion(f32[2048,2048]{1,0:T(8,128)} %fusion.92, bf16[1024,2048]{1,0:T(8,128)(2,1)} %get-tuple-element.148, f32[1024]{0:T(1024)S(1)} %add_rsqrt_fusion, f32[1024]{0:T(1024)S(1)} %get-tuple-element.149, f32[2048]{0:T(1024)S(1)} %bitcast.254, f32[2048]{0:T(1024)S(1)} %bitcast.235, ...), kind=kOutput, calls=%fused_computation.4 | convolution fusion | flops 8610906112 | bytes 33579008 | tf_op jit(solution)/shard_map/md,mf->df/dot_general | solution.py:210
  321.9 13.6 %fusion.199 = f32[1024,2048,1,1]{1,0,3,2:T(8,128)} fusion(bf16[2048,2,3,256]{3,0,2,1:T(8,128)(2,1)} %all-gather.11.cloned.1.call-done, f32[1024,2,1,256]{3,0,2,1:T(8,128)} %bitcast.208, f32[1024,2,1,256]{3,0,2,1:T(8,128)} %bitcast.211, f32[1024,2,1,256]{3,0,2,1:T(8,128)} %bitcast.214), kind=kOutput, calls=%fused_computation.264 | convolution fusion | flops 6445596672 | bytes 20971520 | tf_op jit(solution)/shard_map/mhkc,dhkc->md/dot_general | solution.py:242
  335.5 11.4 %fusion.196 = f32[1024,2048,1,1]{1,0,3,2:T(8,128)} fusion(bf16[2048,2,3,256]{3,0,2,1:T(8,128)(2,1)} %all-gather.11.cloned.1.call-done, f32[1024,2,1,256]{3,0,2,1:T(8,128)S(1)} %bitcast.199, f32[1024,2,1,256]{3,0,2,1:T(8,128)S(1)} %bitcast.203, f32[1024,2,1,256]{3,0,2,1:T(8,128)S(1)} %bitcast.206), kind=kOutput, calls=%fused_computation.263 | convolution fusion | flops 6445596672 | bytes 20971520 | tf_op jit(solution)/shard_map/mhkc,dhkc->md/dot_general | solution.py:242
  347.0 11.7 %fusion.118 = f32[2048,2048]{1,0:T(8,128)} fusion(bf16[1024,2048]{1,0:T(8,128)(2,1)S(1)} %copy-done.60, bf16[2048,2048]{1,0:T(8,128)(2,1)S(1)} %bitcast.177), kind=kOutput, calls=%fused_computation.160 | convolution fusion | flops 8589934592 | bytes 25165824 | tf_op jit(solution)/shard_map/md,mf->df/dot_general | solution.py:204
  358.6 16.5 %fusion.64 = bf16[2048,2048]{0,1:T(8,128)(2,1)} fusion(f32[2048,2048]{1,0:T(8,128)} %fusion.118, bf16[1024,2048]{1,0:T(8,128)(2,1)} %get-tuple-element.136, bf16[2048,2048]{1,0:T(8,128)(2,1)S(1)} %bitcast.177), kind=kOutput, calls=%fused_computation.80 | convolution fusion | flops 8598323200 | bytes 33554432 | tf_op jit(solution)/shard_map/md,mf->df/dot_general | solution.py:204
  375.2 15.0 %fusion.94 = f32[1024,2048]{1,0:T(8,128)} fusion(bf16[2048,2048]{1,0:T(8,128)(2,1)} %all-gather.15.cloned.1.call-done, bf16[1024,2048]{1,0:T(8,128)(2,1)} %copy-done.62), kind=kOutput, calls=%fused_computation.140 | convolution fusion | flops 8589934592 | bytes 20971520 | tf_op jit(solution)/shard_map/mf,df->md/dot_general | solution.py:211
  390.2 30.2 %fusion.34 = (bf16[2048]{0:T(1024)(128)(2,1)S(1)}, f32[1024]{0:T(1024)S(1)}, f32[1024]{0:T(1024)S(1)}, bf16[2048]{0:T(1024)(128)(2,1)S(1)}, f32[1024]{0:T(1024)S...) fusion(f32[1024]{0:T(1024)S(1)} %add_rsqrt_fusion, ...), kind=kOutput, calls=%fused_computation.50 | convolution fusion | flops 8661213184 | bytes 54624256 | tf_op jit(solution)/shard_map/mf,df->md/dot_general | solution.py:211
  420.5 12.5 %fusion.217 = f32[1024,2048]{1,0:T(8,128)S(1)} fusion(bf16[1024,2048]{1,0:T(8,128)(2,1)S(1)} %copy-done.61, bf16[2048,2048]{1,0:T(8,128)(2,1)} %all-gather.17.cloned.1.call-done), kind=kOutput, calls=%fused_computation.277 | convolution fusion | flops 8589934592 | bytes 20971520 | tf_op jit(solution)/shard_map/mf,df->md/dot_general | solution.py:149
  437.4 14.8 %fusion.218 = f32[1024,2048]{1,0:T(8,128)} fusion(bf16[1024,2048]{1,0:T(8,128)(2,1)} %get-tuple-element.136, bf16[2048,2048]{1,0:T(8,128)(2,1)} %all-gather.17.cloned.1.call-done), kind=kOutput, calls=%fused_computation.278 | convolution fusion | flops 8589934592 | bytes 20971520 | tf_op jit(solution)/shard_map/mf,df->md/dot_general | solution.py:149
  452.2 8.5 fusion.65
  460.8 8.4 fusion.44
  487.1 9.2 all-gather.4
  501.3 26.1 %all-reduce.5 = (f32[2,3,256]{2,1,0:T(4,128)S(1)}, f32[2048]{0:T(1024)}) all-reduce(f32[2,3,256]{2,1,0:T(4,128)S(1)} %add.284, f32[2048]{0:T(1024)S(1)} %add.290), channel_id=1, replica_groups=mesh['shard'=8,'tensor'=4] {'shard'}, use_global_device_ids=true, to_apply=%region_37.38 | all-reduce | flops 3584 | bytes 28672 | tf_op jit(solution)/shard_map/psum | solution.py:348
  528.2 21.2 %all-reduce.7 = (bf16[4,2048]{1,0:T(4,128)(2,1)S(1)}, bf16[4,2048]{1,0:T(4,128)(2,1)S(1)}) all-reduce(bf16[4,2048]{1,0:T(4,128)(2,1)S(1)} %pad_maximum_fusion.13, bf16[4,2048]{1,0:T(4,128)(2,1)S(1)} %pad_maximum_fusion.12), channel_id=1, replica_groups=mesh['shard'=8,'tensor'=4] {'tensor'}, use_global_device_ids=true, to_apply=%region_31.32 | all-reduce | flops 16384 | bytes 65536 | tf_op jit(solution)/shard_map/psum | solution.py:331
  558.1 481.4 %all-reduce.11.cloned.1.call-done = (bf16[1024,2048]{1,0:T(8,128)(2,1)}, bf16[1024,2048]{1,0:T(8,128)(2,1)}, bf16[1024,2048]{1,0:T(8,128)(2,1)}, bf16[1024,2048]{1,0:T(8,128)(2,1)}) async-done(((bf16[1024,2048]{1,0:T(8,128)(2,1)}, bf16[1024,2048]{1,0:T(8,128)(2,1)}, bf16[1024,2048]{1,0:T(8,128)(2,1)}, bf16[1024,2048]{1,0:T(8,128)(2,1)}), (bf16[1024,2048]{1,0:T(8,128)(2,1)}, bf16[1024,2048]{1,0:T(8,128)(2,1)}, ...) | async-done | bytes 16777232 | tf_op jit(solution)/shard_map/psum | solution.py:311
  1039.5 11.3 %convert_reduce_fusion.2 = (f32[2048]{0:T(1024)S(1)}, f32[2048]{0:T(1024)S(1)}, f32[1024,2048]{1,0:T(8,128)}, f32[1024,2048]{1,0:T(8,128)}) fusion(bf16[2048,2048]{1,0:T(8,128)(2,1)} %param.27, bf16[1024,2048]{1,0:T(8,128)(2,1)} %get-tuple-element.99, bf16[1024,2048]{1,0:T(8,128)(2,1)} %get-tuple-element.100), kind=kLoop, calls=%fused_computation.14 | loop fusion | flops 16773120 | bytes 33570816 | tf_op jit(solution)/shard_map/reduce_sum | solution.py:202
  1050.8 23.8 %all-reduce.6 = (bf16[2048]{0:T(1024)(128)(2,1)S(1)}, bf16[2048]{0:T(1024)(128)(2,1)S(1)}, bf16[2048]{0:T(1024)(128)(2,1)S(1)}, bf16[2048]{0:T(1024)(128)(2,1)S(1)}, bf16[2048]{0:T(1024)(128)(2,1)S(1)}) all-reduce(bf16[2048]{0:T(1024)(128)(2,1)S(1)} %get-tuple-element.87, ...), channel_id=2, replica_groups=mesh['shard'=8,'tensor'=4] {'shard'}, use_global_device_ids=true, to_apply=%region_32.33.clone | all-reduce | flops 10240 | bytes 40960
  1077.2 10.2 fusion.51
  1087.4 8.5 pad_maximum_fusion.1
  1096.0 11.8 %pad_maximum_fusion = f32[2048,2048]{1,0:T(8,128)} fusion(f32[1024,2048]{1,0:T(8,128)} %get-tuple-element.103, f32[1024,2048]{1,0:T(8,128)} %get-tuple-element.104), kind=kLoop, calls=%fused_computation.2 | loop fusion | flops 4194304 | bytes 33554432 | tf_op jit(solution)/shard_map/concatenate | solution.py:351
  (311 shorter events, 169.3 us)
Async XLA Ops:
  7.2 43.0 %copy-start.45 = (bf16[2048]{0:T(1024)(128)(2,1)S(1)}, bf16[2048]{0:T(1024)(128)(2,1)}, u32[]{:S(2)}) copy-start(bf16[2048]{0:T(1024)(128)(2,1)} %param.24) | copy-start | bytes 12292
  7.2 43.6 %copy-start.47 = (bf16[2,3,256]{2,0,1:T(2,128)(2,1)S(1)}, bf16[2,3,256]{2,0,1:T(2,128)(2,1)}, u32[]{:S(2)}) copy-start(bf16[2,3,256]{2,0,1:T(2,128)(2,1)} %param.18) | copy-start | bytes 9220
  7.2 53.1 %all-gather.13.cloned.1.call-start = ((), (), s32[]{:S(2)}) async-start(), calls=%async_computation.5 | async-start | bytes 2359296 | tf_op jit(solution)/shard_map/all_gather | solution.py:298
  9.0 80.0 %all-gather.11.cloned.1.call-start = ((), (), s32[]{:S(2)}) async-start(), calls=%async_computation.4 | async-start | bytes 7077888 | tf_op jit(solution)/shard_map/all_gather | solution.py:297
  11.2 209.7 %all-gather.15.cloned.1.call-start = ((), (), s32[]{:S(2)}) async-start(), calls=%async_computation.6 | async-start | bytes 9437184 | tf_op jit(solution)/shard_map/all_gather | solution.py:299
  11.9 241.2 %all-gather.17.cloned.1.call-start = ((), (), s32[]{:S(2)}) async-start(), calls=%async_computation.7 | async-start | bytes 9437184 | tf_op jit(solution)/shard_map/all_gather | solution.py:300
  12.5 486.9 %reduce-scatter.7.cloned.1.call-start = ((), (), s32[]{:S(2)}) async-start(), calls=%async_computation.9 | async-start | bytes 2359296 | tf_op jit(solution)/shard_map/reduce_scatter | solution.py:346
  50.2 155.3 %copy-start.39 = (f32[8,1,256]{2,1,0:T(1,128)}, f32[8,1,256]{2,1,0:T(1,128)S(1)}, u32[]{:S(2)}) copy-start(f32[8,1,256]{2,1,0:T(1,128)S(1)} %convert_element_type.304) | copy-start | bytes 24580
  177.8 371.8 %reduce-scatter.5.cloned.1.call-start = ((), (), s32[]{:S(2)}) async-start(), calls=%async_computation.8 | async-start | bytes 7077888 | tf_op jit(solution)/shard_map/reduce_scatter | solution.py:346
  205.5 15.3 %copy-start.15 = (f32[4,256,2,256]{3,1,0,2:T(8,128)}, f32[4,256,2,256]{3,1,0,2:T(8,128)S(1)}, u32[]{:S(2)}) copy-start(f32[4,256,2,256]{3,1,0,2:T(8,128)S(1)} %copy.141) | copy-start | bytes 6291460
  220.8 331.9 %reduce-scatter.9.cloned.1.call-start = ((), (), s32[]{:S(2)}) async-start(), calls=%async_computation.10 | async-start | bytes 9437184 | tf_op jit(solution)/shard_map/reduce_scatter | solution.py:346
  221.5 16.0 %copy-start.43 = (f32[2048]{0:T(1024)S(1)}, f32[2048]{0:T(1024)}, u32[]{:S(2)}) copy-start(f32[2048]{0:T(1024)} %convert_element_type.246) | copy-start | bytes 24580
  221.5 16.0 %copy-start.49 = (bf16[2048,2048]{1,0:T(8,128)(2,1)S(1)}, bf16[2048,2048]{1,0:T(8,128)(2,1)}, u32[]{:S(2)}) copy-start(bf16[2048,2048]{1,0:T(8,128)(2,1)} %all-gather.15.cloned.1.call-done) | copy-start | bytes 25165828
  271.5 16.8 %copy-start.62 = (bf16[1024,2048]{1,0:T(8,128)(2,1)}, bf16[1024,2048]{1,0:T(8,128)(2,1)S(1)}, u32[]{:S(2)}) copy-start(bf16[1024,2048]{1,0:T(8,128)(2,1)S(1)} %get-tuple-element.146) | copy-start | bytes 12582916
  271.5 16.8 %copy-start.48 = (bf16[2048,2048]{1,0:T(8,128)(2,1)S(1)}, bf16[2048,2048]{1,0:T(8,128)(2,1)}, u32[]{:S(2)}) copy-start(bf16[2048,2048]{1,0:T(8,128)(2,1)} %all-gather.17.cloned.1.call-done) | copy-start | bytes 25165828
  271.5 33.4 %slice-start.2 = ((s8[8388608]{0:T(1024)(128)(4,1)}), s8[4194304]{0:T(1024)(128)(4,1)S(1)}, s32[]{:S(2)}) async-start(s8[8388608]{0:T(1024)(128)(4,1)} %bitcast.170), calls=%async_computation.15 | async-start | bytes 8388608
  288.3 16.6 %slice-start.3 = ((s8[8388608]{0:T(1024)(128)(4,1)}), s8[4194304]{0:T(1024)(128)(4,1)S(1)}, s32[]{:S(2)}) async-start(s8[8388608]{0:T(1024)(128)(4,1)} %bitcast.170), calls=%async_computation.16 | async-start | bytes 8388608
  321.8 233.7 %reduce-scatter.11.cloned.1.call-start = ((), (), s32[]{:S(2)}) async-start(), calls=%async_computation.11 | async-start | bytes 9437184 | tf_op jit(solution)/shard_map/reduce_scatter | solution.py:346
  321.8 25.1 %slice-start.8 = ((s8[8388608]{0:T(1024)(128)(4,1)}), s8[4194304]{0:T(1024)(128)(4,1)S(1)}, s32[]{:S(2)}) async-start(s8[8388608]{0:T(1024)(128)(4,1)} %bitcast.176), calls=%async_computation.21 | async-start | bytes 8388608
  375.1 15.0 %copy-start.40 = (f32[8,1,256]{2,1,0:T(1,128)S(1)}, f32[8,1,256]{2,1,0:T(1,128)}, u32[]{:S(2)}) copy-start(f32[8,1,256]{2,1,0:T(1,128)} %copy-done.39) | copy-start | bytes 24580
  375.1 664.3 %all-reduce.11.cloned.1.call-start = ((), (), s32[]{:S(2)}) async-start(), calls=%async_computation.12 | async-start | bytes 33554432 | tf_op jit(solution)/shard_map/psum | solution.py:311
  390.2 30.3 %copy-start.61 = (bf16[1024,2048]{1,0:T(8,128)(2,1)S(1)}, bf16[1024,2048]{1,0:T(8,128)(2,1)}, u32[]{:S(2)}) copy-start(bf16[1024,2048]{1,0:T(8,128)(2,1)} %get-tuple-element.135) | copy-start | bytes 12582916
  433.0 27.7 %slice-start.4 = ((s8[8388608]{0:T(1024)(128)(4,1)}), s8[4194304]{0:T(1024)(128)(4,1)S(1)}, s32[]{:S(2)}) async-start(s8[8388608]{0:T(1024)(128)(4,1)} %bitcast.172), calls=%async_computation.17 | async-start | bytes 8388608
  433.1 27.7 %slice-start.14 = ((s8[8388608]{0:T(1024)(128)(4,1)}), s8[4194304]{0:T(1024)(128)(4,1)S(1)}, s32[]{:S(2)}) async-start(s8[8388608]{0:T(1024)(128)(4,1)} %bitcast.196), calls=%async_computation.27 | async-start | bytes 8388608
  437.4 23.3 %slice-start.5 = ((s8[8388608]{0:T(1024)(128)(4,1)}), s8[4194304]{0:T(1024)(128)(4,1)S(1)}, s32[]{:S(2)}) async-start(s8[8388608]{0:T(1024)(128)(4,1)} %bitcast.172), calls=%async_computation.18 | async-start | bytes 8388608
  437.4 23.3 %slice-start.15 = ((s8[8388608]{0:T(1024)(128)(4,1)}), s8[4194304]{0:T(1024)(128)(4,1)S(1)}, s32[]{:S(2)}) async-start(s8[8388608]{0:T(1024)(128)(4,1)} %bitcast.196), calls=%async_computation.28 | async-start | bytes 8388608
  452.2 16.9 %slice-start.12 = ((s8[8388608]{0:T(1024)(128)(4,1)}), s8[4194304]{0:T(1024)(128)(4,1)S(1)}, s32[]{:S(2)}) async-start(s8[8388608]{0:T(1024)(128)(4,1)} %bitcast.194), calls=%async_computation.25 | async-start | bytes 8388608
  477.3 19.1 %copy-start.8 = (f32[4,256,2,256]{3,1,0,2:T(8,128)S(1)}, f32[4,256,2,256]{3,1,0,2:T(8,128)}, u32[]{:S(2)}) copy-start(f32[4,256,2,256]{3,1,0,2:T(8,128)} %copy.133) | copy-start | bytes 6291460
  479.2 19.8 %copy-start.12 = (f32[4,256,2,256]{3,1,0,2:T(8,128)S(1)}, f32[4,256,2,256]{3,1,0,2:T(8,128)}, u32[]{:S(2)}) copy-start(f32[4,256,2,256]{3,1,0,2:T(8,128)} %copy-done.11) | copy-start | bytes 6291460
  479.2 19.8 %copy-start.14 = (f32[4,256,2,256]{3,1,0,2:T(8,128)S(1)}, f32[4,256,2,256]{3,1,0,2:T(8,128)}, u32[]{:S(2)}) copy-start(f32[4,256,2,256]{3,1,0,2:T(8,128)} %copy-done.13) | copy-start | bytes 6291460
  479.2 19.8 %copy-start.16 = (f32[4,256,2,256]{3,1,0,2:T(8,128)S(1)}, f32[4,256,2,256]{3,1,0,2:T(8,128)}, u32[]{:S(2)}) copy-start(f32[4,256,2,256]{3,1,0,2:T(8,128)} %copy-done.15) | copy-start | bytes 6291460
  1075.3 32.5 %copy-start.46 = (f32[256]{0:T(256)}, f32[256]{0:T(256)S(1)}, u32[]{:S(2)}) copy-start(f32[256]{0:T(256)S(1)} %dynamic-slice_convert_fusion.2) | copy-start | bytes 3076
  (58 other events, 314.7 us)
Sparse Core Ops, SparseCore 0:
  10.5 30.5 all-gather.12
  43.6 45.3 all-gather.10
  90.9 54.2 all-gather.14
  146.9 54.2 all-gather.16
  204.3 41.1 reduce-scatter.6
  248.7 61.5 reduce-scatter.4
  321.9 71.3 reduce-scatter.8
  396.8 71.2 reduce-scatter.10
  477.4 562.0 all-reduce.10
where the time goes:
time: 1120 us
  waiting for transfers between devices  500 us (45%)
  matrix products  340 us (30%)
  blocking collectives  125 us (11%)
  other arithmetic  87.2 us (8%)
  local copies, waits for them, and re-layouts  47.4 us (4%)
  between operations  16.2 us (1%)
    psum x1, waiting for transfers between devices, per_device(): lax.psum(partial_value.astype(jnp.bfloat16), 'tensor').astype(jnp.float32)  481 us
    dot_general x2, matrix products, backward_pass(): jnp.einsum('mf,df->md', d_pre_b, fc1_full, preferred_element_type=jnp.flo...  45.1 us
    dot_general x2, matrix products, backward_pass(): jnp.dot(grad_block, fc2_full, preferred_element_type=jnp.float32)  35 us
    dot_general x2, matrix products, backward_pass(): jnp.einsum('md,mf->df', normed_two, d_pre_b, preferred_element_type=jnp.f...  33.6 us
    dot_general x2, matrix products, backward_pass(): jnp.einsum('md,mhkc->dhkc', normed_one, d_qkv_b, preferred_element_type=j...  30 us
    dot_general x2, matrix products, forward_pass(): jnp.dot(normed_two, fc1_full, preferred_element_type=jnp.float32)  28.4 us
    unnamed x180, local copies, waits for them, and re-layouts  28.2 us
    dot_general x2, matrix products, backward_pass(): jnp.einsum('md,mf->df', grad_block, hidden, preferred_element_type=jnp.fl...  28.2 us
  transfers between devices with their start and end apart: 9, of which 2 were waited for; matrix products, arithmetic and copies ran while one was open for 37% of the time, Pallas kernels for 0%

commit v1 on v0

--- a/solution.py
+++ b/solution.py
@@ -308,7 +308,9 @@
         partial_value, saved = forward_pass(
             x_block, forward_weights, qkv_bias, fc1_bias, cos_tab, sin_tab
         )
-        branch_total = lax.psum(partial_value.astype(jnp.bfloat16), "tensor").astype(jnp.float32)
+        branch_total = jnp.sum(
+            lax.all_gather(partial_value.astype(jnp.bfloat16), "tensor"), axis=0
+        ).astype(jnp.float32)
         shifts = forward_weights[8].astype(jnp.float32) + forward_weights[9].astype(jnp.float32)
         outputs.append((saved[0] + branch_total + shifts).astype(jnp.bfloat16))
         backward_weights = (

time: 1120 us -> 1410 us (1.26)
  waiting for transfers between devices: 500 us -> 762 us
  other arithmetic: 87.2 us -> 119 us
    all_gather x0 -> x2, waiting for transfers between devices: none -> 265 us  [per_device(): lax.all_gather(partial_value.astype(jnp.bfloat16), 'tensor')]
    psum x1, waiting for transfers between devices: 481 us -> 282 us  [per_device(): lax.psum(d_input.astype(jnp.bfloat16), 'tensor').astype(jnp.float32)]
    reduce_scatter x4, waiting for transfers between devices: 0.05 us -> 168 us  [per_device(): lax.psum_scatter(as_sent(grad_accum), 'shard', scatter_dimension=0, tiled...]
    reduce_sum x0 -> x2, other arithmetic: none -> 25.6 us  [per_device(): jnp.sum(lax.all_gather(partial_value.astype(jnp.bfloat16), 'tensor'), axi...]
    all_gather x1, waiting for transfers between devices: 0.01 us -> 20.8 us  [per_device(): lax.all_gather(own_shards[3], 'shard', axis=0, tiled=True)]
    unnamed x180 -> x182, local copies, waits for them, and re-layouts: 28.2 us -> 33 us
  transfers between devices with their start and end apart: 9 -> 11, of which waited for: 2 -> 8; matrix products, arithmetic and copies ran while one was open for 37% -> 31% of each run, Pallas kernels for 0% -> 0%
where the time goes in v1:
time: 1410 us; the launch traced here: 1400 us
  waiting for transfers between devices  762 us (54%)
  matrix products  334 us (24%)
  blocking collectives  120 us (9%)
  other arithmetic  119 us (8%)
  local copies, waits for them, and re-layouts  47.4 us (3%)
  between operations  16 us (1%)
    psum x1, waiting for transfers between devices, per_device(): lax.psum(d_input.astype(jnp.bfloat16), 'tensor').astype(jnp.float32)  282 us
    all_gather x2, waiting for transfers between devices, per_device(): lax.all_gather(partial_value.astype(jnp.bfloat16), 'tensor')  265 us
    reduce_scatter x4, waiting for transfers between devices, per_device(): lax.psum_scatter(as_sent(grad_accum), 'shard', scatter_dimension=0, tiled...  168 us
    dot_general x2, matrix products, backward_pass(): jnp.einsum('mf,df->md', d_pre_b, fc1_full, preferred_element_type=jnp.flo...  39.3 us
    dot_general x2, matrix products, backward_pass(): jnp.dot(grad_block, fc2_full, preferred_element_type=jnp.float32)  35.5 us
    unnamed x182, local copies, waits for them, and re-layouts  33 us
    dot_general x2, matrix products, backward_pass(): jnp.einsum('md,mf->df', normed_two, d_pre_b, preferred_element_type=jnp.f...  31.8 us
    dot_general x2, matrix products, backward_pass(): jnp.einsum('md,mf->df', grad_block, hidden, preferred_element_type=jnp.fl...  31.5 us
  transfers between devices with their start and end apart: 11, of which 8 were waited for; matrix products, arithmetic and copies ran while one was open for 31% of the time, Pallas kernels for 0%

profile of v1, /device:TPU:0, one launch (start us, length us, event | category | flops | bytes accessed | tf_op | source)
XLA Modules:
  0.0 1399.3 jit_solution(8799751059579448121)
XLA Ops:
  64.5 24.5 %all-gather.15.cloned.1.call-done = bf16[2048,2,3,256]{3,0,2,1:T(8,128)(2,1)} async-done(((bf16[256,2,3,256]{3,0,2,1:T(8,128)(2,1)}), bf16[2048,2,3,256]{3,0,2,1:T(8,128)(2,1)}) %all-gather.15.cloned.1.call-update) | async-done | bytes 6291472 | tf_op jit(solution)/shard_map/all_gather | solution.py:297
  89.0 11.5 broadcast_add_fusion
  148.6 12.8 fusion.209
  164.6 15.8 %multiply_convert_fusion.1 = (bf16[1024,2048]{1,0:T(8,128)(2,1)}, bf16[1024,2048]{1,0:T(8,128)(2,1)}, f32[1024,2048]{1,0:T(8,128)}) fusion(f32[2048]{0:T(1024)S(1)} %convert_element_type.250, f32[1024,2048]{1,0:T(8,128)S(1)} %fusion.209, bf16[2048,2048]{1,0:T(8,128)(2,1)S(1)} %copy-done.61, f32[2048]{0:T(1024)S(1)} %bitcast.232, f32[2048]{0:T(1024)S(1)} %bitcast.213, ...), kind=kOutput, calls=%fused_computation.92 | convolution fusion | flops 8627683328 | bytes 37781504 | tf_op jit(solution)/shard_map/dot_general | solution.py:142
  180.4 20.8 %all-gather.21.cloned.1.call-done = bf16[2048,2048]{1,0:T(8,128)(2,1)} async-done(((bf16[256,2048]{1,0:T(8,128)(2,1)}), bf16[2048,2048]{1,0:T(8,128)(2,1)}) %all-gather.21.cloned.1.call-update) | async-done | bytes 8388624 | tf_op jit(solution)/shard_map/all_gather | solution.py:300
  201.2 12.7 fusion.218
  221.9 11.4 fusion.217
  277.0 14.8 %fusion.146 = f32[2048,2,3,256]{3,0,2,1:T(8,128)} fusion(f32[2048]{0:T(1024)S(1)} %bitcast.237, f32[2048]{0:T(1024)S(1)} %bitcast.221, f32[1024]{0:T(1024)S(1)} %add_rsqrt_fusion.1, f32[1024]{0:T(1024)S(1)} %broadcast_multiply_fusion.9, f32[1024,2,1,256]{3,0,2,1:T(8,128)} %bitcast.178, f32[1024,2,1,256]{3,0,2,1:T(8,128)} %bitcast.181, ...), kind=kOutput, calls=%fused_computation.178 | convolution fusion | flops 6464471040 | bytes 23093248 | tf_op jit(solution)/shard_map/md,mhkc->dhkc/dot_general | solution.py:239
  304.6 15.3 %add_convert_fusion.2 = bf16[2048,2,3,256]{3,0,2,1:T(8,128)(2,1)} fusion(f32[2048,2,3,256]{3,0,2,1:T(8,128)} %fusion.146, f32[1024]{0:T(1024)S(1)} %add_rsqrt_fusion, f32[1024]{0:T(1024)S(1)} %broadcast_multiply_fusion.8, f32[2048]{0:T(1024)S(1)} %bitcast.238, f32[2048]{0:T(1024)S(1)} %bitcast.222, f32[1024,2,1,256]{3,0,2,1:T(8,128)S(1)} %bitcast.187, ...), kind=kOutput, calls=%fused_computation.5 | convolution fusion | flops 6470762496 | bytes 29384704 | tf_op jit(solution)/shard_map/md,mhkc->dhkc/dot_general | solution.py:239
  319.9 16.8 %fusion.215 = (f32[2048]{0:T(1024)}, bf16[1024,2048]{1,0:T(8,128)(2,1)S(1)}) fusion(f32[1024,2048]{1,0:T(8,128)} %get-tuple-element.138, f32[2048]{0:T(1024)S(1)} %convert_element_type.250, bf16[2048,2048]{1,0:T(8,128)(2,1)} %all-gather.21.cloned.1.call-done, bf16[2048,2048]{1,0:T(8,128)(2,1)} %param.27), kind=kOutput, calls=%fused_computation.275 | convolution fusion | flops 8615098368 | bytes 25182208 | tf_op jit(solution)/shard_map/dot_general | solution.py:207
  338.7 15.1 %fusion.92 = f32[2048,2048]{1,0:T(8,128)} fusion(bf16[1024,2048]{1,0:T(8,128)(2,1)S(1)} %get-tuple-element.145, f32[2048]{0:T(1024)S(1)} %bitcast.233, f32[2048]{0:T(1024)S(1)} %bitcast.214, f32[1024]{0:T(1024)S(1)} %add_rsqrt_fusion.1, f32[1024]{0:T(1024)S(1)} %broadcast_multiply_fusion.9, bf16[2048,2048]{1,0:T(8,128)(2,1)} %param.14), kind=kOutput, calls=%fused_computation.138 | convolution fusion | flops 8602517504 | bytes 25190400 | tf_op jit(solution)/shard_map/md,mf->df/dot_general | solution.py:210
  353.8 18.7 %fusion.216 = (f32[2048]{0:T(1024)}, bf16[1024,2048]{1,0:T(8,128)(2,1)}) fusion(f32[1024,2048]{1,0:T(8,128)} %copy-done.72, f32[2048]{0:T(1024)S(1)} %convert_element_type.250, bf16[2048,2048]{1,0:T(8,128)(2,1)} %all-gather.21.cloned.1.call-done, bf16[2048,2048]{1,0:T(8,128)(2,1)} %param.27), kind=kOutput, calls=%fused_computation.276 | convolution fusion | flops 8615098368 | bytes 25182208 | tf_op jit(solution)/shard_map/dot_general | solution.py:207
  372.5 16.7 %add_convert_fusion.1 = bf16[2048,2048]{1,0:T(8,128)(2,1)} fusion(f32[2048,2048]{1,0:T(8,128)} %fusion.92, bf16[1024,2048]{1,0:T(8,128)(2,1)} %get-tuple-element.147, f32[1024]{0:T(1024)S(1)} %add_rsqrt_fusion, f32[1024]{0:T(1024)S(1)} %broadcast_multiply_fusion.8, f32[2048]{0:T(1024)S(1)} %bitcast.234, f32[2048]{0:T(1024)S(1)} %bitcast.215, ...), kind=kOutput, calls=%fused_computation.4 | convolution fusion | flops 8610906112 | bytes 33579008 | tf_op jit(solution)/shard_map/md,mf->df/dot_general | solution.py:210
  407.0 15.7 %fusion.118 = f32[2048,2048]{1,0:T(8,128)} fusion(bf16[1024,2048]{1,0:T(8,128)(2,1)} %get-tuple-element.134, bf16[2048,2048]{1,0:T(8,128)(2,1)} %param.27), kind=kOutput, calls=%fused_computation.160 | convolution fusion | flops 8589934592 | bytes 25165824 | tf_op jit(solution)/shard_map/md,mf->df/dot_general | solution.py:204
  422.7 15.8 %fusion.64 = bf16[2048,2048]{0,1:T(8,128)(2,1)} fusion(f32[2048,2048]{1,0:T(8,128)} %fusion.118, bf16[1024,2048]{1,0:T(8,128)(2,1)S(1)} %copy-done.71, bf16[2048,2048]{1,0:T(8,128)(2,1)} %param.27), kind=kOutput, calls=%fused_computation.80 | convolution fusion | flops 8598323200 | bytes 33554432 | tf_op jit(solution)/shard_map/md,mf->df/dot_general | solution.py:204
  438.6 13.0 fusion.199
  462.7 11.1 fusion.94
  473.8 28.2 %fusion.34 = (bf16[2048]{0:T(1024)(128)(2,1)S(1)}, f32[1024]{0:T(1024)S(1)}, f32[1024]{0:T(1024)S(1)}, bf16[2048]{0:T(1024)(128)(2,1)S(1)}, f32[1024]{0:T(1024)S...) fusion(f32[1024]{0:T(1024)S(1)} %add_rsqrt_fusion, ...), kind=kOutput, calls=%fused_computation.50 | convolution fusion | flops 8661213184 | bytes 54624256 | tf_op jit(solution)/shard_map/mf,df->md/dot_general | solution.py:211
  502.1 11.2 fusion.30
  513.3 13.4 reduce_sum.301
  526.7 265.0 %all-gather.23.cloned.1.call-done = bf16[4096,2048]{1,0:T(8,128)(2,1)} async-done(((bf16[1024,2048]{1,0:T(8,128)(2,1)}), bf16[4096,2048]{1,0:T(8,128)(2,1)}) %all-gather.23.cloned.1.call-update) | async-done | bytes 16777232 | tf_op jit(solution)/shard_map/all_gather | solution.py:312
  791.7 12.2 reduce_sum.297
  803.9 19.1 %fusion.51 = (bf16[1024,2048]{1,0:T(8,128)(2,1)}, bf16[1024,2048]{1,0:T(8,128)(2,1)}, bf16[1024,2048]{1,0:T(8,128)(2,1)}) fusion(bf16[1024,2048]{1,0:T(8,128)(2,1)} %reduce_sum.297, f32[2048]{0:T(1024)S(1)} %bitcast.226, bf16[2048,2048]{1,0:T(8,128)(2,1)} %param.14, bf16[1024,2048]{1,0:T(8,128)(2,1)} %reduce_sum.301, f32[1024]{0:T(1024)S(1)} %broadcast_multiply_fusion.4, ...), kind=kLoop, calls=%fused_computation.67 | loop fusion | flops 48234496 | bytes 46186496 | tf_op jit(solution)/shard_map/convert_element_type | solution.py:315
  836.2 23.5 %all-reduce.5 = (f32[2,3,256]{2,1,0:T(4,128)S(1)}, f32[2048]{0:T(1024)}) all-reduce(f32[2,3,256]{2,1,0:T(4,128)S(1)} %add.280, f32[2048]{0:T(1024)S(1)} %add.286), channel_id=1, replica_groups=mesh['shard'=8,'tensor'=4] {'shard'}, use_global_device_ids=true, to_apply=%region_37.38 | all-reduce | flops 3584 | bytes 28672 | tf_op jit(solution)/shard_map/psum | solution.py:350
  860.5 19.0 %all-reduce.7 = (bf16[4,2048]{1,0:T(4,128)(2,1)S(1)}, bf16[4,2048]{1,0:T(4,128)(2,1)S(1)}) all-reduce(bf16[4,2048]{1,0:T(4,128)(2,1)S(1)} %pad_maximum_fusion.13, bf16[4,2048]{1,0:T(4,128)(2,1)S(1)} %pad_maximum_fusion.12), channel_id=1, replica_groups=mesh['shard'=8,'tensor'=4] {'tensor'}, use_global_device_ids=true, to_apply=%region_31.32 | all-reduce | flops 16384 | bytes 65536 | tf_op jit(solution)/shard_map/psum | solution.py:333
  879.7 19.7 %reduce-scatter.5.cloned.1.call-done = bf16[256,2,3,256]{3,0,2,1:T(8,128)(2,1)} async-done(((bf16[2048,2,3,256]{3,0,2,1:T(8,128)(2,1)}), bf16[256,2,3,256]{3,0,2,1:T(8,128)(2,1)}) %reduce-scatter.5.cloned.1.call-update) | async-done | bytes 786448 | tf_op jit(solution)/shard_map/reduce_scatter | solution.py:348
  902.4 71.9 %reduce-scatter.9.cloned.1.call-done = bf16[256,2048]{1,0:T(8,128)(2,1)} async-done(((bf16[2048,2048]{1,0:T(8,128)(2,1)}), bf16[256,2048]{1,0:T(8,128)(2,1)}) %reduce-scatter.9.cloned.1.call-update) | async-done | bytes 1048592 | tf_op jit(solution)/shard_map/reduce_scatter | solution.py:348
  977.1 71.8 %reduce-scatter.11.cloned.1.call-done = bf16[256,2048]{0,1:T(8,128)(2,1)} async-done(((bf16[2048,2048]{0,1:T(8,128)(2,1)}), bf16[256,2048]{0,1:T(8,128)(2,1)}) %reduce-scatter.11.cloned.1.call-update) | async-done | bytes 1048592 | tf_op jit(solution)/shard_map/reduce_scatter | solution.py:348
  1060.0 282.4 %all-reduce.11.cloned.1.call-done = (bf16[1024,2048]{1,0:T(8,128)(2,1)}, bf16[1024,2048]{1,0:T(8,128)(2,1)}) async-done(((bf16[1024,2048]{1,0:T(8,128)(2,1)}, bf16[1024,2048]{1,0:T(8,128)(2,1)}), (bf16[1024,2048]{1,0:T(8,128)(2,1)}, bf16[1024,2048]{1,0:T(8,128)(2,1)})) %all-reduce.11.cloned.1.call-update) | async-done | bytes 8388624 | tf_op jit(solution)/shard_map/psum | solution.py:332
  1342.4 11.3 convert_reduce_fusion.2
  1353.7 23.8 %all-reduce.6 = (bf16[2048]{0:T(1024)(128)(2,1)S(1)}, bf16[2048]{0:T(1024)(128)(2,1)S(1)}, bf16[2048]{0:T(1024)(128)(2,1)S(1)}, bf16[2048]{0:T(1024)(128)(2,1)S(1)}, bf16[2048]{0:T(1024)(128)(2,1)S(1)}) all-reduce(bf16[2048]{0:T(1024)(128)(2,1)S(1)} %get-tuple-element.87, ...), channel_id=4, replica_groups=mesh['shard'=8,'tensor'=4] {'shard'}, use_global_device_ids=true, to_apply=%region_32.33.clone | all-reduce | flops 10240 | bytes 40960
  1380.2 11.8 pad_maximum_fusion
  (318 shorter events, 236.5 us)
Async XLA Ops:
  7.2 42.0 %copy-start.58 = (bf16[2048]{0:T(1024)(128)(2,1)S(1)}, bf16[2048]{0:T(1024)(128)(2,1)}, u32[]{:S(2)}) copy-start(bf16[2048]{0:T(1024)(128)(2,1)} %param.24) | copy-start | bytes 12292
  7.2 42.0 %copy-start.60 = (bf16[2,3,256]{2,0,1:T(2,128)(2,1)S(1)}, bf16[2,3,256]{2,0,1:T(2,128)(2,1)}, u32[]{:S(2)}) copy-start(bf16[2,3,256]{2,0,1:T(2,128)(2,1)} %param.18) | copy-start | bytes 9220
  7.2 52.0 %all-gather.17.cloned.1.call-start = ((), (), s32[]{:S(2)}) async-start(), calls=%async_computation.5 | async-start | bytes 2359296 | tf_op jit(solution)/shard_map/all_gather | solution.py:298
  9.0 80.0 %all-gather.15.cloned.1.call-start = ((), (), s32[]{:S(2)}) async-start(), calls=%async_computation.4 | async-start | bytes 7077888 | tf_op jit(solution)/shard_map/all_gather | solution.py:297
  11.2 137.4 %all-gather.19.cloned.1.call-start = ((), (), s32[]{:S(2)}) async-start(), calls=%async_computation.6 | async-start | bytes 9437184 | tf_op jit(solution)/shard_map/all_gather | solution.py:299
  11.9 189.3 %all-gather.21.cloned.1.call-start = ((), (), s32[]{:S(2)}) async-start(), calls=%async_computation.7 | async-start | bytes 9437184 | tf_op jit(solution)/shard_map/all_gather | solution.py:300
  12.5 500.8 %all-gather.25.cloned.1.call-start = ((), (), s32[]{:S(2)}) async-start(), calls=%async_computation.13 | async-start | bytes 20971520 | tf_op jit(solution)/shard_map/all_gather | solution.py:312
  23.1 138.3 %copy-start.54 = (f32[8,1,256]{2,1,0:T(1,128)}, f32[8,1,256]{2,1,0:T(1,128)S(1)}, u32[]{:S(2)}) copy-start(f32[8,1,256]{2,1,0:T(1,128)S(1)} %convert_element_type.311) | copy-start | bytes 24580
  32.1 129.3 %copy-start.47 = (f32[8,1,256]{2,1,0:T(1,128)}, f32[8,1,256]{2,1,0:T(1,128)S(1)}, u32[]{:S(2)}) copy-start(f32[8,1,256]{2,1,0:T(1,128)S(1)} %convert_element_type.310) | copy-start | bytes 24580
  40.3 67.9 %copy-start.56 = (f32[8,1,256]{2,1,0:T(1,128)}, f32[8,1,256]{2,1,0:T(1,128)S(1)}, u32[]{:S(2)}) copy-start(f32[8,1,256]{2,1,0:T(1,128)S(1)} %convert_element_type.309) | copy-start | bytes 24580
  49.2 58.9 %copy-start.49 = (f32[8,1,256]{2,1,0:T(1,128)}, f32[8,1,256]{2,1,0:T(1,128)S(1)}, u32[]{:S(2)}) copy-start(f32[8,1,256]{2,1,0:T(1,128)S(1)} %convert_element_type.308) | copy-start | bytes 24580
  59.2 77.9 %copy-start.29 = (f32[256,32]{1,0:T(8,128)}, f32[256,32]{1,0:T(8,128)S(1)}, u32[]{:S(2)}) copy-start(f32[256,32]{1,0:T(8,128)S(1)} %get-tuple-element.136) | copy-start | bytes 98308
  59.2 77.9 %copy-start.31 = (f32[256,32]{1,0:T(8,128)}, f32[256,32]{1,0:T(8,128)S(1)}, u32[]{:S(2)}) copy-start(f32[256,32]{1,0:T(8,128)S(1)} %get-tuple-element.137) | copy-start | bytes 98308
  64.5 58.9 %copy-start.24 = (bf16[1024,2,256]{2,0,1:T(8,128)(2,1)}, bf16[1024,2,256]{2,0,1:T(8,128)(2,1)S(1)}, u32[]{:S(2)}) copy-start(bf16[1024,2,256]{2,0,1:T(8,128)(2,1)S(1)} %fusion.134) | copy-start | bytes 3145732
  148.6 16.0 %copy-start.61 = (bf16[2048,2048]{1,0:T(8,128)(2,1)S(1)}, bf16[2048,2048]{1,0:T(8,128)(2,1)}, u32[]{:S(2)}) copy-start(bf16[2048,2048]{1,0:T(8,128)(2,1)} %all-gather.19.cloned.1.call-done) | copy-start | bytes 25165828
  218.4 573.3 %all-gather.23.cloned.1.call-start = ((), (), s32[]{:S(2)}) async-start(), calls=%async_computation.12 | async-start | bytes 20971520 | tf_op jit(solution)/shard_map/all_gather | solution.py:312
  237.7 596.6 %reduce-scatter.7.cloned.1.call-start = ((), (), s32[]{:S(2)}) async-start(), calls=%async_computation.9 | async-start | bytes 2359296 | tf_op jit(solution)/shard_map/reduce_scatter | solution.py:348
  276.9 622.5 %reduce-scatter.5.cloned.1.call-start = ((), (), s32[]{:S(2)}) async-start(), calls=%async_computation.8 | async-start | bytes 7077888 | tf_op jit(solution)/shard_map/reduce_scatter | solution.py:348
  276.9 14.8 %copy-start.34 = (bf16[4,256,2,192]{3,1,2,0:T(8,128)(2,1)S(1)}, bf16[4,256,2,192]{3,1,2,0:T(8,128)(2,1)}, u32[]{:S(2)}) copy-start(bf16[4,256,2,192]{3,1,2,0:T(8,128)(2,1)} %slice.350) | copy-start | bytes 2359300
  304.5 15.3 %copy-start.16 = (f32[4,256,2,256]{3,1,0,2:T(8,128)}, f32[4,256,2,256]{3,1,0,2:T(8,128)S(1)}, u32[]{:S(2)}) copy-start(f32[4,256,2,256]{3,1,0,2:T(8,128)S(1)} %copy.141) | copy-start | bytes 6291460
  319.9 654.5 %reduce-scatter.9.cloned.1.call-start = ((), (), s32[]{:S(2)}) async-start(), calls=%async_computation.10 | async-start | bytes 9437184 | tf_op jit(solution)/shard_map/reduce_scatter | solution.py:348
  319.9 18.8 %copy-start.48 = (f32[8,1,256]{2,1,0:T(1,128)S(1)}, f32[8,1,256]{2,1,0:T(1,128)}, u32[]{:S(2)}) copy-start(f32[8,1,256]{2,1,0:T(1,128)} %copy-done.47) | copy-start | bytes 24580
  319.9 18.8 %copy-start.55 = (f32[8,1,256]{2,1,0:T(1,128)S(1)}, f32[8,1,256]{2,1,0:T(1,128)}, u32[]{:S(2)}) copy-start(f32[8,1,256]{2,1,0:T(1,128)} %copy-done.54) | copy-start | bytes 24580
  338.7 33.8 %slice-start.2 = ((s8[8388608]{0:T(1024)(128)(4,1)}), s8[4194304]{0:T(1024)(128)(4,1)S(1)}, s32[]{:S(2)}) async-start(s8[8388608]{0:T(1024)(128)(4,1)} %bitcast.168), calls=%async_computation.17 | async-start | bytes 8388608
  353.8 18.7 %slice-start.3 = ((s8[8388608]{0:T(1024)(128)(4,1)}), s8[4194304]{0:T(1024)(128)(4,1)S(1)}, s32[]{:S(2)}) async-start(s8[8388608]{0:T(1024)(128)(4,1)} %bitcast.168), calls=%async_computation.18 | async-start | bytes 8388608
  389.3 659.7 %reduce-scatter.11.cloned.1.call-start = ((), (), s32[]{:S(2)}) async-start(), calls=%async_computation.11 | async-start | bytes 9437184 | tf_op jit(solution)/shard_map/reduce_scatter | solution.py:348
  407.0 15.7 %copy-start.71 = (bf16[1024,2048]{1,0:T(8,128)(2,1)S(1)}, bf16[1024,2048]{1,0:T(8,128)(2,1)}, u32[]{:S(2)}) copy-start(bf16[1024,2048]{1,0:T(8,128)(2,1)} %get-tuple-element.135) | copy-start | bytes 12582916
  438.5 13.1 copy-start.9
  438.6 903.9 %all-reduce.11.cloned.1.call-start = ((), (), s32[]{:S(2)}) async-start(), calls=%async_computation.14 | async-start | bytes 16777216 | tf_op jit(solution)/shard_map/psum | solution.py:332
  438.6 13.1 copy-start.10
  438.6 24.1 %slice-start.4 = ((s8[8388608]{0:T(1024)(128)(4,1)}), s8[4194304]{0:T(1024)(128)(4,1)S(1)}, s32[]{:S(2)}) async-start(s8[8388608]{0:T(1024)(128)(4,1)} %bitcast.239), calls=%async_computation.19 | async-start | bytes 8388608
  1378.3 13.8 copy-start.59
  (63 other events, 309.0 us)
Sparse Core Ops, SparseCore 0:
  10.5 30.5 all-gather.16
  43.6 45.3 all-gather.14
  90.9 54.2 all-gather.18
  146.9 54.2 all-gather.20
  218.5 286.7 all-gather.24
  506.7 284.9 all-gather.22
  795.0 39.2 reduce-scatter.6
  837.7 61.6 reduce-scatter.4
  902.8 71.4 reduce-scatter.8
  977.6 71.2 reduce-scatter.10
  1051.6 290.8 all-reduce.10
